TPU v7x, 32 devices: a whole 2x2x4 slice. The times are simulated.
32 devices in a mesh: subj: 4 (over y, core), vox: 8 (over z, x).
Axes of the slice: x: 2, y: 2, z: 4, core: 2. Of those that a mesh axis runs over, the one named last changes fastest.
Arguments:
- series: bfloat16 [16, 256, 16384], P('subj', None, 'vox'), may hold values from -6 to 6
- offsets: int32 [16, 12], replicated, may hold values from 0 to 240
- selected: int32 [16], replicated, may hold values from 0 to 16383, as said below
Outputs:
- kernel: float32 [16, 192, 192], P('vox', 'subj')
Inputs may be any that keep to these rules, and one draw needn't show every extreme that they name: `offsets`: each epoch lies inside its subject's run; epochs may intersect. `selected`: the ids are distinct.
All inputs are finite; a program needn't handle non-finite values.
Results may differ from a plain program's by a relative error of at most 0.00035.
Values may be sent and summed in bfloat16 or wider, within the bound.
A program may use at most 128 MiB of HBM per device.

v0:
```python
import functools

import jax
import jax.numpy as jnp
from jax import lax
from jax.experimental import pallas as pl
from jax.experimental.pallas import tpu as pltpu
from jax.sharding import PartitionSpec as P

TR = 16
KB = 8
C1 = 4
series_floor = 1.0
spread_floor = 0.05
shrink_factor = 0.9
f32 = jnp.float32
bf16 = jnp.bfloat16


def iota(shape, dim):
    return lax.broadcasted_iota(jnp.int32, shape, dim)


def pieces_of(G, V, NE):
    R = V
    while R > G and (V % R or R % G or (G * NE) % R or (G * NE // R) % 8):
        R -= 1
    return R


def kernel(
    G, V, NS, EP, SEL, W,
    off_ref, sel_ref, series_hbm, out_ref,
    series_ref, load_sem, ep, hot, inv, part, slots, a_hi, a_lo, perm, send, recv,
    gram, pieces_in, summed, landed,
    slab_send, slab_recv, sc_send, sc_recv, rs_send, rs_recv, fin_send, fin_recv,
):
    subj = lax.axis_index("subj")
    vox = lax.axis_index("vox")
    RUN = series_ref.shape[1]
    VL = series_ref.shape[2]
    ROWS = EP * TR
    H = SEL // KB
    KH = KB // G
    SL = SEL // V
    NE = NS * EP
    chunks = VL // W
    R = pieces_of(G, V, NE)
    VR = V // R
    RP = G * NE // R
    PG = R // G
    ORDER = tuple(range(G // 2, G)) + tuple(range(1, G // 2))

    barrier = pltpu.get_barrier_semaphore()
    for d in range(1, G):
        pl.semaphore_signal(
            barrier, inc=1, device_id=(lax.rem(subj + d, G), vox),
            device_id_type=pl.DeviceIdType.MESH,
        )
    for d in range(1, V):
        pl.semaphore_signal(
            barrier, inc=1, device_id=(subj, lax.rem(vox + d, V)),
            device_id_type=pl.DeviceIdType.MESH,
        )

    def load(s):
        return pltpu.make_async_copy(series_hbm.at[s], series_ref.at[s], load_sem.at[s])

    for s in range(NS):
        load(s).start()

    ids = jnp.zeros((SEL, 1), jnp.int32)
    which = iota((SEL, 1), 0)
    for p in range(SEL):
        ids = jnp.where(which == p, sel_ref[(p % V) * SL + p // V], ids)
    picker = jnp.where(iota((SEL, VL), 1) + vox * VL == ids, 1.0, 0.0).astype(bf16)
    col = iota((TR, RUN), 1) - iota((TR, RUN), 0)
    pieces = []
    for s in range(NS):
        tiles = [
            jnp.where(col == off_ref[subj * NS + s, e], 1.0, 0.0) for e in range(EP)
        ]
        hot[s] = jnp.concatenate(tiles, axis=0).astype(bf16)
    for s in range(NS):
        load(s).wait()
        runs = lax.dot_general(
            picker, series_ref[s], (((1,), (1,)), ((), ())), preferred_element_type=f32
        )
        pieces.append(lax.dot_general(
            runs.astype(bf16), hot[s], (((1,), (1,)), ((), ())), preferred_element_type=f32
        ))
    joined = jnp.concatenate(pieces, axis=1)
    for h in range(H):
        part[h] = joined[h * KB:(h + 1) * KB].astype(bf16)

    def gather(c, carry):
        at = pl.ds(pl.multiple_of(c * W, W), W)
        for s in range(NS):
            x = jnp.dot(hot[s], series_ref[s, :, at], preferred_element_type=f32)
            ep[s, :, at] = x.astype(bf16)
            x3 = x.reshape(EP, TR, W)
            total = jnp.sum(x3, axis=1)
            ssq = jnp.sum(x3 * x3, axis=1) - total * total * (1.0 / TR)
            inv[s, :, at] = shrink_factor * lax.rsqrt(jnp.maximum(ssq, 0.0) + series_floor)
        return carry

    after = chunks * C1 // 8
    pl.semaphore_wait(barrier, G + V - 2)

    def slab_copy(h, d, sender):
        return pltpu.make_async_remote_copy(
            src_ref=part.at[h], dst_ref=slots.at[h, sender],
            send_sem=slab_send.at[h, d], recv_sem=slab_recv.at[h, d],
            device_id=(subj, lax.rem(vox + d, V)),
            device_id_type=pl.DeviceIdType.MESH,
        )

    for h in range(H):
        for d in range(1, V):
            slab_copy(h, d, vox).start()

    out_row = iota((KB * NE, KB * NE), 0)
    in_row = iota((KB * NE, KB * NE), 1)
    slot = out_row // NE
    source = lax.rem(out_row, NE) * KB + lax.rem(slot, KH) * G + slot // KH
    perm[...] = jnp.where(source == in_row, 1.0, 0.0).astype(bf16)

    lax.fori_loop(0, after, gather, 0)

    same = iota((ROWS, ROWS), 0) // TR == iota((ROWS, ROWS), 1) // TR
    ones = jnp.where(same, 1.0, 0.0)
    pick_e = iota((EP, KB, ROWS), 2) // TR == iota((EP, KB, ROWS), 0)

    def slab_rows(h):
        slab = part[h].astype(f32)
        for d in range(1, V):
            slab_copy(h, d, lax.rem(vox - d + V, V)).wait_recv()
        for d in range(1, V):
            slab = slab + slots[h, lax.rem(vox + d, V)].astype(f32)
        rows = jnp.concatenate(
            [slab[:, s * ROWS:(s + 1) * ROWS] for s in range(NS)], axis=0
        )
        mean = jnp.dot(
            rows.astype(bf16), ones.astype(bf16), preferred_element_type=f32
        ) * (1.0 / TR)
        centred = rows - mean
        ssq = jnp.dot(
            centred * centred, ones,
            precision=lax.Precision.HIGHEST, preferred_element_type=f32,
        )
        std = centred / jnp.sqrt(ssq + series_floor)
        hi = std.astype(bf16).astype(f32)
        lo = std - hi
        for s in range(NS):
            for value, where in ((hi, a_hi), (lo, a_lo)):
                block = value[s * KB:(s + 1) * KB]
                spread = jnp.where(pick_e, block[None], 0.0).reshape(EP * KB, ROWS)
                where[h, s] = spread.astype(bf16)

    every = pl.ds(0, VL)

    def score_copy(h, i, n, d, sender, at):
        return pltpu.make_async_remote_copy(
            src_ref=send.at[h, lax.rem(subj + d, G), pl.ds(i, n), :, at],
            dst_ref=recv.at[h, pl.ds(i, n), pl.ds(pl.multiple_of(sender * NE, NE), NE), at],
            send_sem=sc_send.at[h, i, d], recv_sem=sc_recv.at[h, i, d],
            device_id=(lax.rem(subj + d, G), vox),
            device_id_type=pl.DeviceIdType.MESH,
        )

    def groups(h):
        return ((0, KH),) if h == 0 else tuple((i, 1) for i in range(KH))

    own_rows = pl.ds(pl.multiple_of(subj * NE, NE), NE)
    for h in range(H):
        slab_rows(h)

        def scores(c, carry, h=h):
            if h == 0 and after < chunks:
                @pl.when(c >= after)
                def _():
                    gather(c, 0)

            at = pl.ds(pl.multiple_of(c * W, W), W)
            parts = []
            for s in range(NS):
                x = ep[s, :, at]
                corr = jnp.dot(a_hi[h, s], x, preferred_element_type=f32)
                corr = corr + jnp.dot(a_lo[h, s], x, preferred_element_type=f32)
                r = corr.reshape(EP, KB, W) * inv[s, :, at][:, None, :]
                f = 0.5 * (jnp.log(1.0 + r) - jnp.log(1.0 - r))
                f = f - jnp.sum(f, axis=0, keepdims=True) * (1.0 / EP)
                var = jnp.sum(f * f, axis=0, keepdims=True) * (1.0 / EP)
                z = f * lax.rsqrt(var + spread_floor)
                parts.append(z.reshape(EP * KB, W).astype(bf16))
            z = jnp.concatenate(parts, axis=0)
            moved = jnp.dot(perm[...], z, preferred_element_type=f32)
            send[h, :, :, :, at] = moved.astype(bf16).reshape(G, KH, NE, W)
            if h == 0:
                for d in ORDER:
                    score_copy(h, 0, KH, d, subj, at).start()
            recv[h, :, own_rows, at] = send[h, subj, :, :, at]
            return carry

        lax.fori_loop(0, chunks, scores, 0)

        if h:
            for i, n in groups(h):
                for d in ORDER:
                    score_copy(h, i, n, d, subj, every).start()

    def row_piece(r):
        return pl.ds(pl.multiple_of(r * RP, RP), RP)

    def part_copy(t, d):
        to = lax.rem(vox + d, V)
        return pltpu.make_async_remote_copy(
            src_ref=gram.at[t, row_piece(to // VR)], dst_ref=pieces_in.at[t, d - 1],
            send_sem=rs_send.at[t, d], recv_sem=rs_recv.at[t],
            device_id=(subj, to), device_id_type=pl.DeviceIdType.MESH,
        )

    def all_parts(t):
        return pltpu.make_async_remote_copy(
            src_ref=pieces_in.at[t], dst_ref=pieces_in.at[t],
            send_sem=rs_send.at[t, 0], recv_sem=rs_recv.at[t],
            device_id=(subj, lax.rem(vox + 1, V)), device_id_type=pl.DeviceIdType.MESH,
        )

    piece = vox // VR
    to_subj = piece // PG
    to_rows = lax.rem(piece, PG)

    def reduces(v):
        return lax.rem(v, VR) == 0

    def spot(t):
        p = t * G + subj
        return lax.rem(p, V), p // V

    def final_copy(t):
        owner, local = spot(t)
        return pltpu.make_async_remote_copy(
            src_ref=summed.at[t], dst_ref=landed.at[local, to_rows],
            send_sem=fin_send.at[t], recv_sem=fin_recv.at[local, to_rows],
            device_id=(to_subj, owner), device_id_type=pl.DeviceIdType.MESH,
        )

    def away(t):
        owner, local = spot(t)
        return jnp.logical_or(to_subj != subj, owner != vox)

    def finish(t):
        @pl.when(reduces(vox))
        def _():
            all_parts(t).wait_recv()
            total = gram[t, row_piece(piece)]
            for d in range(1, V):
                total = total + pieces_in[t, d - 1]
            total = total * (1.0 / (VL * V))
            summed[t] = total

            @pl.when(away(t))
            def _():
                final_copy(t).start()

            @pl.when(jnp.logical_not(away(t)))
            def _():
                landed[spot(t)[1], to_rows] = total

    T = H * KH
    for h in range(H):
        for i in range(KH):
            t = h * KH + i
            for first, n in groups(h):
                if first == i:
                    for d in range(1, G):
                        sender = lax.rem(subj - d + G, G)
                        score_copy(h, i, n, d, sender, every).wait_recv()
            rows = recv[h, i]
            gram[t] = lax.dot_general(
                rows, rows, (((1,), (1,)), ((), ())), preferred_element_type=f32
            )
            for d in range(1, V):
                @pl.when(reduces(lax.rem(vox + d, V)))
                def _():
                    part_copy(t, d).start()
            if t:
                finish(t - 1)
    finish(T - 1)

    for local in range(SL):
        p = local * V + vox
        handler = lax.rem(p, G)
        for b in range(PG):
            source = (subj * PG + b) * VR

            @pl.when(jnp.logical_or(handler != subj, source != vox))
            def _():
                pltpu.make_async_remote_copy(
                    src_ref=summed.at[0], dst_ref=landed.at[local, b],
                    send_sem=fin_send.at[0], recv_sem=fin_recv.at[local, b],
                    device_id=(subj, lax.rem(vox + 1, V)),
                    device_id_type=pl.DeviceIdType.MESH,
                ).wait_recv()
            out_ref[local, b * RP:(b + 1) * RP] = landed[local, b]

    for h in range(H):
        for d in range(1, V):
            slab_copy(h, d, vox).wait_send()
        for i, n in groups(h):
            for d in range(1, G):
                score_copy(h, i, n, d, subj, every).wait_send()
    for t in range(T):
        for d in range(1, V):
            @pl.when(reduces(lax.rem(vox + d, V)))
            def _():
                part_copy(t, d).wait_send()

        @pl.when(jnp.logical_and(reduces(vox), away(t)))
        def _():
            final_copy(t).wait_send()


def body(series, offsets, selected):
    G = lax.axis_size("subj")
    V = lax.axis_size("vox")
    NS, RUN, VL = series.shape
    EP = offsets.shape[1]
    SEL = selected.shape[0]
    W = 256
    NE = NS * EP
    ROWS = EP * TR
    H = SEL // KB
    KH = KB // G
    SL = SEL // V
    R = pieces_of(G, V, NE)
    RP = G * NE // R
    vm = pltpu.VMEM
    dma = pltpu.SemaphoreType.DMA
    return pl.pallas_call(
        functools.partial(kernel, G, V, NS, EP, SEL, W),
        out_shape=jax.ShapeDtypeStruct((SL, NE, G * NE), f32),
        in_specs=[
            pl.BlockSpec(memory_space=pltpu.SMEM),
            pl.BlockSpec(memory_space=pltpu.SMEM),
            pl.BlockSpec(memory_space=pl.ANY),
        ],
        out_specs=pl.BlockSpec(memory_space=pltpu.VMEM),
        scratch_shapes=[
            vm((NS, RUN, VL), bf16),
            dma((NS,)),
            vm((NS, ROWS, VL), bf16),
            vm((NS, ROWS, RUN), bf16),
            vm((NS, EP, VL), f32),
            vm((H, KB, NS * ROWS), bf16),
            vm((H, V, KB, NS * ROWS), bf16),
            vm((H, NS, EP * KB, ROWS), bf16),
            vm((H, NS, EP * KB, ROWS), bf16),
            vm((KB * NE, KB * NE), bf16),
            vm((H, G, KH, NE, VL), bf16),
            vm((H, KH, G * NE, VL), bf16),
            vm((H * KH, G * NE, G * NE), f32),
            vm((H * KH, V - 1, RP, G * NE), f32),
            vm((H * KH, RP, G * NE), f32),
            vm((SL, R // G, RP, G * NE), f32),
            dma((H, V)),
            dma((H, V)),
            dma((H, KH, G)),
            dma((H, KH, G)),
            dma((H * KH, V)),
            dma((H * KH,)),
            dma((H * KH,)),
            dma((SL, R // G)),
        ],
        compiler_params=pltpu.CompilerParams(
            collective_id=0, has_side_effects=True, vmem_limit_bytes=56 * 1024 * 1024
        ),
    )(offsets, selected, series)


def solution(mesh):
    placed = (P("subj", None, "vox"), P(), P())
    return jax.shard_map(
        body, mesh=mesh, in_specs=placed, out_specs=P("vox", "subj", None), check_vma=False
    )
```

profile of v0, /device:TPU:21, one launch (start us, length us, event | category | flops | bytes accessed | tf_op | source)
XLA Modules:
  0.0 59.3 jit_solution(11215177106066046716)
XLA Ops:
  0.0 57.7 %shard_map.37 = f32[2,48,192]{2,1,0:T(8,128)} custom-call(s32[16,12]{1,0:T(8,128)} %off_ref.1, s32[16]{0:T(128)} %sel_ref.1, bf16[4,256,2048]{2,1,0:T(8,128)(2,1)} %series_hbm.1), custom_call_target="tpu_custom_call" | custom-call | tf_op jit(solution)/shard_map/pallas_call | solution.py:341
  57.7 1.5 %copy.5 = f32[2,48,192]{2,1,0:T(8,128)} copy(f32[2,48,192]{2,1,0:T(8,128)} %shard_map.37) | data formatting | bytes 147456
where the time goes:
time: 59.5 us; the launch traced here: 59.3 us
  Pallas kernels  57.7 us (97%)
  local copies, waits for them, and re-layouts  1.54 us (3%)
    pallas_call x1, Pallas kernels, body(): pl.pallas_call(functools.partial(kernel, G, V, NS, EP, SEL, W), out_shape...  57.7 us
    unnamed x1, local copies, waits for them, and re-layouts  1.54 us

commit v1 on v0

--- a/solution.py
+++ b/solution.py
@@ -21,6 +21,10 @@
     return lax.broadcasted_iota(jnp.int32, shape, dim)
 
 
+def up8(n):
+    return -(-n // 8) * 8
+
+
 def pieces_of(G, V, NE):
     R = V
     while R > G and (V % R or R % G or (G * NE) % R or (G * NE // R) % 8):
@@ -32,8 +36,9 @@
     G, V, NS, EP, SEL, W,
     off_ref, sel_ref, series_hbm, out_ref,
     series_ref, load_sem, ep, hot, inv, part, slots, a_hi, a_lo, perm, send, recv,
-    gram, pieces_in, summed, landed,
-    slab_send, slab_recv, sc_send, sc_recv, rs_send, rs_recv, fin_send, fin_recv,
+    expand, gram, pieces_in, summed, landed, direct,
+    slab_send, slab_recv, sc_send, sc_recv, last_send, last_recv,
+    rs_send, rs_recv, fin_send, fin_recv, dir_send, dir_recv,
 ):
     subj = lax.axis_index("subj")
     vox = lax.axis_index("vox")
@@ -49,7 +54,18 @@
     VR = V // R
     RP = G * NE // R
     PG = R // G
-    ORDER = tuple(range(G // 2, G)) + tuple(range(1, G // 2))
+    T = H * KH
+    E1 = EP - 1
+    NR = NS * E1
+    BR = send.shape[2]
+    starts = tuple(i * NR // 8 * 8 for i in range(KH))
+    HG = G // 2
+    shift = V // 2 + G // 2
+    half = subj // HG
+    cross = [(1 - half) * HG + b for b in range(HG)]
+    near = [half * HG + lax.rem(subj + d, HG) for d in range(1, HG)]
+    Q = last_recv.shape[0] - 1
+    QC = VL // Q
 
     barrier = pltpu.get_barrier_semaphore()
     for d in range(1, G):
@@ -72,7 +88,7 @@
     ids = jnp.zeros((SEL, 1), jnp.int32)
     which = iota((SEL, 1), 0)
     for p in range(SEL):
-        ids = jnp.where(which == p, sel_ref[(p % V) * SL + p // V], ids)
+        ids = jnp.where(which == p, sel_ref[(p + shift) % V * SL + p // V], ids)
     picker = jnp.where(iota((SEL, VL), 1) + vox * VL == ids, 1.0, 0.0).astype(bf16)
     col = iota((TR, RUN), 1) - iota((TR, RUN), 0)
     pieces = []
@@ -119,11 +135,21 @@
         for d in range(1, V):
             slab_copy(h, d, vox).start()
 
-    out_row = iota((KB * NE, KB * NE), 0)
-    in_row = iota((KB * NE, KB * NE), 1)
-    slot = out_row // NE
-    source = lax.rem(out_row, NE) * KB + lax.rem(slot, KH) * G + slot // KH
-    perm[...] = jnp.where(source == in_row, 1.0, 0.0).astype(bf16)
+    out_row = iota((G * BR, 1), 0)
+    within = lax.rem(out_row, BR)
+    item = lax.rem(within, NR)
+    source = (item // E1 * EP + lax.rem(item, E1)) * KB + within // NR * G + out_row // BR
+    source = jnp.where(within < KH * NR, source, -1)
+    perm[...] = jnp.where(source == iota((G * BR, KB * NE), 1), 1.0, 0.0).astype(bf16)
+
+    full_row = iota((G * NE, 1), 0)
+    epoch = lax.rem(full_row, EP)
+    for i in range(KH):
+        first = full_row // NE * NE + i * NR - starts[i] + lax.rem(full_row, NE) // EP * E1
+        at = iota((G * NE, G * NE), 1) - first
+        keep = jnp.where(at == epoch, 1.0, 0.0)
+        rest = jnp.where(jnp.logical_and(at >= 0, at < E1), -1.0, 0.0)
+        expand[i] = jnp.where(epoch < E1, keep, rest).astype(bf16)
 
     lax.fori_loop(0, after, gather, 0)
 
@@ -159,19 +185,31 @@
 
     every = pl.ds(0, VL)
 
-    def score_copy(h, i, n, d, sender, at):
-        return pltpu.make_async_remote_copy(
-            src_ref=send.at[h, lax.rem(subj + d, G), pl.ds(i, n), :, at],
-            dst_ref=recv.at[h, pl.ds(i, n), pl.ds(pl.multiple_of(sender * NE, NE), NE), at],
-            send_sem=sc_send.at[h, i, d], recv_sem=sc_recv.at[h, i, d],
-            device_id=(lax.rem(subj + d, G), vox),
-            device_id_type=pl.DeviceIdType.MESH,
-        )
-
-    def groups(h):
-        return ((0, KH),) if h == 0 else tuple((i, 1) for i in range(KH))
-
-    own_rows = pl.ds(pl.multiple_of(subj * NE, NE), NE)
+    def score_copy(h, to, sender, at):
+        return pltpu.make_async_remote_copy(
+            src_ref=send.at[h, to, :, at], dst_ref=recv.at[h, sender, :, at],
+            send_sem=sc_send.at[h, to], recv_sem=sc_recv.at[h, sender],
+            device_id=(to, vox), device_id_type=pl.DeviceIdType.MESH,
+        )
+
+    top = NE if KH > 1 else 0
+    head_rows, tail_rows = pl.ds(0, top), pl.ds(top, BR - top)
+
+    def last_copy(n, to, sender, at):
+        rows = tail_rows if n < Q else head_rows
+        return pltpu.make_async_remote_copy(
+            src_ref=send.at[H - 1, to, rows, at], dst_ref=recv.at[H - 1, sender, rows, at],
+            send_sem=last_send.at[n, to], recv_sem=last_recv.at[n, sender],
+            device_id=(to, vox), device_id_type=pl.DeviceIdType.MESH,
+        )
+
+    def quarter(n):
+        return pl.ds(n * QC, QC)
+
+    last_parts = tuple((n, quarter(n)) for n in range(Q))
+    if top:
+        last_parts = ((Q, every),) + last_parts
+
     for h in range(H):
         slab_rows(h)
 
@@ -195,19 +233,18 @@
                 parts.append(z.reshape(EP * KB, W).astype(bf16))
             z = jnp.concatenate(parts, axis=0)
             moved = jnp.dot(perm[...], z, preferred_element_type=f32)
-            send[h, :, :, :, at] = moved.astype(bf16).reshape(G, KH, NE, W)
-            if h == 0:
-                for d in ORDER:
-                    score_copy(h, 0, KH, d, subj, at).start()
-            recv[h, :, own_rows, at] = send[h, subj, :, :, at]
+            send[h, :, :, at] = moved.astype(bf16).reshape(G, BR, W)
+            if h < H - 1:
+                for to in cross + near:
+                    score_copy(h, to, subj, at).start()
+            recv[h, subj, :, at] = send[h, subj, :, at]
             return carry
 
         lax.fori_loop(0, chunks, scores, 0)
 
-        if h:
-            for i, n in groups(h):
-                for d in ORDER:
-                    score_copy(h, i, n, d, subj, every).start()
+    for to in near + cross:
+        for n, at in last_parts:
+            last_copy(n, to, subj, at).start()
 
     def row_piece(r):
         return pl.ds(pl.multiple_of(r * RP, RP), RP)
@@ -236,7 +273,7 @@
 
     def spot(t):
         p = t * G + subj
-        return lax.rem(p, V), p // V
+        return lax.rem(p + shift, V), p // V
 
     def final_copy(t):
         owner, local = spot(t)
@@ -268,50 +305,112 @@
             def _():
                 landed[spot(t)[1], to_rows] = total
 
-    T = H * KH
+    others = near + cross
+
+    def add_gram(t, at, fresh):
+        h, i = t // KH, t % KH
+        rows = recv[h, :, starts[i]:starts[i] + NE, at].reshape(G * NE, -1)
+        rows = jnp.dot(expand[i], rows, preferred_element_type=f32).astype(bf16)
+        value = lax.dot_general(
+            rows, rows, (((1,), (1,)), ((), ())), preferred_element_type=f32
+        )
+        gram[t] = value if fresh else gram[t] + value
+
+    for t in range(T - 1):
+        if t % KH == 0 and t < T - KH:
+            for sender in others:
+                score_copy(t // KH, sender, sender, every).wait_recv()
+        if t == T - KH:
+            for sender in others:
+                last_copy(Q, sender, sender, every).wait_recv()
+        for n in range(Q):
+            add_gram(t, quarter(n), n == 0)
+        for d in range(1, V):
+            @pl.when(reduces(lax.rem(vox + d, V)))
+            def _():
+                part_copy(t, d).start()
+        if t:
+            finish(t - 1)
+
+    for n in range(Q):
+        for sender in others:
+            last_copy(n, sender, sender, quarter(n)).wait_recv()
+        add_gram(T - 1, quarter(n), n == 0)
+
+    owner, local = spot(T - 1)
+
+    def block(j):
+        return pl.ds(j * NE, NE)
+
+    def direct_copy(j):
+        return pltpu.make_async_remote_copy(
+            src_ref=gram.at[T - 1, block(j)], dst_ref=direct.at[vox],
+            send_sem=dir_send.at[j], recv_sem=dir_recv.at[vox],
+            device_id=(j, owner), device_id_type=pl.DeviceIdType.MESH,
+        )
+
+    def here(j):
+        return jnp.logical_and(owner == vox, subj == j)
+
+    for j in range(G):
+        @pl.when(jnp.logical_not(here(j)))
+        def _():
+            direct_copy(j).start()
+
+    if T > 1:
+        finish(T - 2)
+
+    for local in range(SL):
+        p = local * V + lax.rem(vox - shift + 2 * V, V)
+        handler = lax.rem(p, G)
+        is_direct = p >= (T - 1) * G
+
+        @pl.when(jnp.logical_not(is_direct))
+        def _():
+            for b in range(PG):
+                source = (subj * PG + b) * VR
+
+                @pl.when(jnp.logical_or(handler != subj, source != vox))
+                def _():
+                    pltpu.make_async_remote_copy(
+                        src_ref=summed.at[0], dst_ref=landed.at[local, b],
+                        send_sem=fin_send.at[0], recv_sem=fin_recv.at[local, b],
+                        device_id=(subj, lax.rem(vox + 1, V)),
+                        device_id_type=pl.DeviceIdType.MESH,
+                    ).wait_recv()
+                out_ref[local, b * RP:(b + 1) * RP] = landed[local, b]
+
+        if (local + 1) * V > (T - 1) * G:
+            @pl.when(is_direct)
+            def _():
+                @pl.when(handler == subj)
+                def _():
+                    direct[vox] = gram[T - 1, pl.ds(pl.multiple_of(subj * NE, NE), NE)]
+
+                for v in range(V):
+                    @pl.when(jnp.logical_or(handler != subj, v != vox))
+                    def _():
+                        pltpu.make_async_remote_copy(
+                            src_ref=direct.at[v], dst_ref=direct.at[v],
+                            send_sem=dir_send.at[0], recv_sem=dir_recv.at[v],
+                            device_id=(subj, lax.rem(vox + 1, V)),
+                            device_id_type=pl.DeviceIdType.MESH,
+                        ).wait_recv()
+                total = direct[0]
+                for v in range(1, V):
+                    total = total + direct[v]
+                out_ref[local] = total * (1.0 / (VL * V))
+
     for h in range(H):
-        for i in range(KH):
-            t = h * KH + i
-            for first, n in groups(h):
-                if first == i:
-                    for d in range(1, G):
-                        sender = lax.rem(subj - d + G, G)
-                        score_copy(h, i, n, d, sender, every).wait_recv()
-            rows = recv[h, i]
-            gram[t] = lax.dot_general(
-                rows, rows, (((1,), (1,)), ((), ())), preferred_element_type=f32
-            )
-            for d in range(1, V):
-                @pl.when(reduces(lax.rem(vox + d, V)))
-                def _():
-                    part_copy(t, d).start()
-            if t:
-                finish(t - 1)
-    finish(T - 1)
-
-    for local in range(SL):
-        p = local * V + vox
-        handler = lax.rem(p, G)
-        for b in range(PG):
-            source = (subj * PG + b) * VR
-
-            @pl.when(jnp.logical_or(handler != subj, source != vox))
-            def _():
-                pltpu.make_async_remote_copy(
-                    src_ref=summed.at[0], dst_ref=landed.at[local, b],
-                    send_sem=fin_send.at[0], recv_sem=fin_recv.at[local, b],
-                    device_id=(subj, lax.rem(vox + 1, V)),
-                    device_id_type=pl.DeviceIdType.MESH,
-                ).wait_recv()
-            out_ref[local, b * RP:(b + 1) * RP] = landed[local, b]
-
-    for h in range(H):
         for d in range(1, V):
             slab_copy(h, d, vox).wait_send()
-        for i, n in groups(h):
-            for d in range(1, G):
-                score_copy(h, i, n, d, subj, every).wait_send()
-    for t in range(T):
+        for to in others:
+            if h < H - 1:
+                score_copy(h, to, subj, every).wait_send()
+            else:
+                for n, at in last_parts:
+                    last_copy(n, to, subj, at).wait_send()
+    for t in range(T - 1):
         for d in range(1, V):
             @pl.when(reduces(lax.rem(vox + d, V)))
             def _():
@@ -320,6 +419,10 @@
         @pl.when(jnp.logical_and(reduces(vox), away(t)))
         def _():
             final_copy(t).wait_send()
+    for j in range(G):
+        @pl.when(jnp.logical_not(here(j)))
+        def _():
+            direct_copy(j).wait_send()
 
 
 def body(series, offsets, selected):
@@ -336,6 +439,8 @@
     SL = SEL // V
     R = pieces_of(G, V, NE)
     RP = G * NE // R
+    BR = up8(KH * NS * (EP - 1))
+    Q = 4
     vm = pltpu.VMEM
     dma = pltpu.SemaphoreType.DMA
     return pl.pallas_call(
@@ -357,21 +462,27 @@
             vm((H, V, KB, NS * ROWS), bf16),
             vm((H, NS, EP * KB, ROWS), bf16),
             vm((H, NS, EP * KB, ROWS), bf16),
-            vm((KB * NE, KB * NE), bf16),
-            vm((H, G, KH, NE, VL), bf16),
-            vm((H, KH, G * NE, VL), bf16),
+            vm((G * BR, KB * NE), bf16),
+            vm((H, G, BR, VL), bf16),
+            vm((H, G, BR, VL), bf16),
+            vm((KH, G * NE, G * NE), bf16),
             vm((H * KH, G * NE, G * NE), f32),
             vm((H * KH, V - 1, RP, G * NE), f32),
             vm((H * KH, RP, G * NE), f32),
             vm((SL, R // G, RP, G * NE), f32),
+            vm((V, NE, G * NE), f32),
             dma((H, V)),
             dma((H, V)),
-            dma((H, KH, G)),
-            dma((H, KH, G)),
+            dma((H, G)),
+            dma((H, G)),
+            dma((Q + 1, G)),
+            dma((Q + 1, G)),
             dma((H * KH, V)),
             dma((H * KH,)),
             dma((H * KH,)),
             dma((SL, R // G)),
+            dma((G,)),
+            dma((V,)),
         ],
         compiler_params=pltpu.CompilerParams(
             collective_id=0, has_side_effects=True, vmem_limit_bytes=56 * 1024 * 1024

time: 59.5 us -> 61.6 us (1.035)
  the two profiles are of different devices: /device:TPU:21 before, /device:TPU:15 now
where the time goes in v1:
time: 61.6 us; the launch traced here: 61.4 us
  Pallas kernels  59.8 us (97%)
  local copies, waits for them, and re-layouts  1.54 us (2%)
    pallas_call x1, Pallas kernels, body(): pl.pallas_call(functools.partial(kernel, G, V, NS, EP, SEL, W), out_shape...  59.8 us
    unnamed x1, local copies, waits for them, and re-layouts  1.54 us

profile of v1, /device:TPU:15, one launch (start us, length us, event | category | flops | bytes accessed | tf_op | source)
XLA Modules:
  0.0 61.4 jit_solution(13030617656741165598)
XLA Ops:
  0.0 59.8 %shard_map.37 = f32[2,48,192]{2,1,0:T(8,128)} custom-call(s32[16,12]{1,0:T(8,128)} %off_ref.1, s32[16]{0:T(128)} %sel_ref.1, bf16[4,256,2048]{2,1,0:T(8,128)(2,1)} %series_hbm.1), custom_call_target="tpu_custom_call" | custom-call | tf_op jit(solution)/shard_map/pallas_call | solution.py:446
  59.8 1.5 %copy.5 = f32[2,48,192]{2,1,0:T(8,128)} copy(f32[2,48,192]{2,1,0:T(8,128)} %shard_map.37) | data formatting | bytes 147456
